TPU v7x, 256 devices: a whole 4x4x8 slice. The times are simulated.
256 devices in a mesh: row: 8 (over x, core), col: 32 (over y, z).
Axes of the slice: x: 4, y: 4, z: 8, core: 2. Of those that a mesh axis runs over, the one named last changes fastest.
Arguments:
- embeddings: bfloat16 [32768, 512], P(('row', 'col')), may hold values from -6 to 6
- sketch: bfloat16 [32768, 64], P(('row', 'col')), may hold values from -240 to 240
Outputs:
- basis: float32 [32768, 64], P(('row', 'col'))
- first_pass: float32 [32768, 64], P(('row', 'col'))
All inputs are finite; a program needn't handle non-finite values.
Results may differ from a plain program's by a relative error of at most 0.00205.
Values may be sent and summed in bfloat16 or wider, within the bound.
A program may use at most 64 MiB of HBM per device.

v0:
```python
import jax
import jax.numpy as jnp
from jax import lax
from jax.sharding import Mesh
from jax.sharding import PartitionSpec as P

ROW = ("row_0", "row_1")
COL = ("col_0", "col_1")
ROW_COL = ("row_0", "row_1", "col_0", "col_1")


def in_order(blocks, dim):
    blocks = jnp.moveaxis(blocks, 0, dim)
    dims = blocks.shape
    return blocks.reshape(*dims[:dim], dims[dim] * dims[dim + 1], *dims[dim + 2 :])


def from_everyone(shard, axis):
    copies = jnp.broadcast_to(shard, (lax.axis_size(axis), *shard.shape))
    return lax.all_to_all(copies, axis, split_axis=0, concat_axis=0, tiled=True)


def gather_directly(shard, axis, dim):
    return in_order(from_everyone(shard, axis), dim)


def in_blocks(shard, dim, length):
    dims = shard.shape
    blocks = shard.reshape(*dims[:dim], length, dims[dim] // length, *dims[dim + 1 :])
    return jnp.moveaxis(blocks, dim, 0)


def sent_and_summed(shard, axis, dim):
    length = lax.axis_size(axis)
    blocks = lax.all_to_all(in_blocks(shard, dim, length), axis, 0, 0, tiled=True)
    return jnp.sum(blocks, axis=0)


def over_copies(shard, axis):
    return from_everyone(shard, axis).sum(axis=0)


def one_axis_at_a_time(shard, axes):
    far, near = axes
    return over_copies(over_copies(shard, near), far)


def squares_of(points):
    return jnp.sum(jnp.square(points.astype(jnp.float32)), axis=1)


def kernel_tile(left, right, left_sq, right_sq, gamma):
    cross = lax.dot_general(
        left, right, (((1,), (1,)), ((), ())), preferred_element_type=jnp.float32
    )
    dist = left_sq[:, None] + right_sq[None, :] - 2.0 * cross
    return jnp.exp(-gamma * dist).astype(jnp.bfloat16)


def product_of(left, right):
    return lax.dot_general(
        left,
        right,
        (((0,), (0,)), ((), ())),
        precision=lax.Precision.HIGHEST,
        preferred_element_type=jnp.float32,
    )


def per_device(embeddings, sketch):
    width = embeddings.shape[1]
    gamma = 3.0 / width
    own_points = gather_directly(embeddings, ROW, 0)
    own_sq = squares_of(own_points)
    empty = jnp.zeros((own_points.shape[0], sketch.shape[1]), jnp.float32)
    total = empty
    points = lax.all_gather(embeddings, COL, axis=0, tiled=True)
    tests = lax.all_gather(sketch, COL, axis=0, tiled=True)
    count = points.shape[0]
    size = 512

    def step(carry, block):
        block_points, block_tests = block
        tile = kernel_tile(own_points, block_points, own_sq, squares_of(block_points), gamma)
        return (carry + jnp.dot(tile, block_tests, preferred_element_type=jnp.float32), None)

    stacked = (
        points.reshape(count // size, size, width),
        tests.reshape(count // size, size, tests.shape[1]),
    )
    total, unused = lax.scan(step, total, stacked)
    sketched = sent_and_summed(total, ROW, 0)
    core = one_axis_at_a_time(
        product_of(sketch.astype(jnp.float32), sketched), (("row_0", "row_1"), ("col_0", "col_1"))
    )
    lower = jnp.linalg.cholesky(core)
    first = jax.scipy.linalg.solve_triangular(lower, sketched.T, lower=True).T
    gram_two = one_axis_at_a_time(
        product_of(first, first), (("row_0", "row_1"), ("col_0", "col_1"))
    )
    lower_two = jnp.linalg.cholesky(gram_two)
    second = jax.scipy.linalg.solve_triangular(lower_two, first.T, lower=True).T
    total_points = sketched.shape[0] * lax.axis_size(ROW) * lax.axis_size(COL)
    scale = jnp.sqrt(jnp.float32(total_points))
    return (second * scale, first * scale)


def solution(mesh):
    torus = Mesh(mesh.devices.reshape(4, 2, 4, 8), ("row_0", "row_1", "col_0", "col_1"))
    in_specs = (P(ROW_COL, None), P(ROW_COL, None))
    out_specs = (P(ROW_COL, None), P(ROW_COL, None))
    return jax.shard_map(
        per_device, mesh=torus, in_specs=in_specs, out_specs=out_specs, check_vma=False
    )
```

profile of v0, /device:TPU:32, one launch (start us, length us, event | category | flops | bytes accessed | tf_op | source)
XLA Modules:
  0.0 239.0 jit_solution(14531047242678938613)
XLA Ops:
  7.9 2.0 broadcast_in_dim.22
  9.9 4.3 %all-to-all-start = ((bf16[8,128,512]{2,1,0:T(8,128)(2,1)}), bf16[8,128,512]{2,1,0:T(8,128)(2,1)S(1)}, u32[]{:S(2)}, u32[]{:S(2)}) async-start(bf16[8,128,512]{2,1,0:T(8,128)(2,1)} %broadcast_in_dim.22), calls=%async_computation | async-start | bytes 2097152 | tf_op jit(solution)/shard_map/all_to_all | solution.py:20
  14.2 52.8 %all_gather.7 = bf16[4096,64]{0,1:T(8,128)(2,1)S(1)} all-gather(bf16[128,64]{0,1:T(8,128)(2,1)S(1)} %copy-done), channel_id=1, replica_groups=mesh['row_0'=4,'row_1'=2,'col_0'=4,'col_1'=8] {'col_0','col_1'}, dimensions={0}, use_global_device_ids=true | all-gather | bytes 540672 | tf_op jit(solution)/shard_map/all_gather | solution.py:78
  67.8 27.1 %all-gather.2.cloned.1.call-done = bf16[4096,512]{1,0:T(8,128)(2,1)} async-done(((bf16[128,512]{1,0:T(8,128)(2,1)}), bf16[4096,512]{1,0:T(8,128)(2,1)}) %all-gather.2.cloned.1.call-update) | async-done | bytes 4194320 | tf_op jit(solution)/shard_map/all_gather | solution.py:77
  94.9 26.7 %while.11 = (s32[]{:T(128)}, f32[1024,64]{0,1:T(8,128)S(1)}, f32[1024]{0:T(1024)S(1)}, bf16[8,512,512]{2,1,0:T(8,128)(2,1)}, bf16[1024,512]{1,0:T(8,128)(2,1)S(1...) while((s32[]{:T(128)}, f32[1024,64]{0,1:T(8,128)S(1)}, f32[1024]{0:T(1024)S(1)}, ...), condition=%wide.region_3.4_spmd.clone, body=%wide.region_1.3_spmd.clone.sunk | while | flops 607518208 | bytes 2761827 | solution.py:91
  96.1 2.1 fusion.45
  99.4 2.1 fusion.45
  102.8 2.1 fusion.45
  106.1 2.1 fusion.45
  109.4 2.1 fusion.45
  112.8 2.1 fusion.45
  116.1 2.1 fusion.45
  119.4 2.1 fusion.45
  121.6 11.6 %all_to_all.30 = f32[8,128,64]{1,2,0:T(8,128)S(1)} all-to-all(f32[8,128,64]{1,2,0:T(8,128)S(1)} %copy_bitcast_fusion), channel_id=1, replica_groups=mesh['row_0'=4,'row_1'=2,'col_0'=4,'col_1'=8] {'row_0','row_1'}, dimensions={0} | all-to-all | bytes 524288 | tf_op jit(solution)/shard_map/all_to_all | solution.py:35
  134.2 22.9 %all_to_all.31 = f32[32,1,4096]{2,1,0:T(1,128)S(1)} all-to-all(f32[32,1,4096]{2,1,0:T(1,128)S(1)} %reshape.31), channel_id=1, replica_groups=mesh['row_0'=4,'row_1'=2,'col_0'=4,'col_1'=8] {'col_0','col_1'}, dimensions={0} | all-to-all | bytes 1048576 | tf_op jit(solution)/shard_map/all_to_all | solution.py:20
  160.3 8.5 %all_to_all.32 = f32[8,1,4096]{2,1,0:T(1,128)S(1)} all-to-all(f32[8,1,4096]{2,1,0:T(1,128)S(1)} %reshape.33), channel_id=1, replica_groups=mesh['row_0'=4,'row_1'=2,'col_0'=4,'col_1'=8] {'row_0','row_1'}, dimensions={0} | all-to-all | bytes 262144 | tf_op jit(solution)/shard_map/all_to_all | solution.py:20
  169.9 5.8 %cholesky.44 = f32[64,64]{1,0:T(8,128)S(1)} custom-call(f32[64,64]{1,0:T(8,128)S(1)} %fusion.27), custom_call_target="Cholesky" | custom-call | tf_op jit(solution)/shard_map/jit(cholesky)/cholesky | solution.py:96
  177.1 4.9 %custom-call.7 = f32[1,64,64]{1,2,0:T(8,128)S(1)} custom-call(f32[1,64,64]{2,1,0:T(8,128)S(1)} %fusion.20), custom_call_target="InvertDiagBlocksLowerTriangular" | custom-call | tf_op jit(solution)/shard_map/jit(_solve_triangular)/triangular_solve | solution.py:97
  183.3 22.1 %all_to_all.33 = f32[32,1,4096]{2,1,0:T(1,128)S(1)} all-to-all(f32[32,1,4096]{2,1,0:T(1,128)S(1)} %reshape.35), channel_id=1, replica_groups=mesh['row_0'=4,'row_1'=2,'col_0'=4,'col_1'=8] {'col_0','col_1'}, dimensions={0} | all-to-all | bytes 1048576 | tf_op jit(solution)/shard_map/all_to_all | solution.py:20
  205.3 1.9 reduce.7
  208.6 3.5 %all-to-all-start.5 = ((f32[8,1,4096]{2,1,0:T(1,128)}), f32[8,1,4096]{2,1,0:T(1,128)S(1)}, u32[]{:S(2)}, u32[]{:S(2)}) async-start(f32[8,1,4096]{2,1,0:T(1,128)} %reshape.37), calls=%async_computation.5 | async-start | bytes 262144 | tf_op jit(solution)/shard_map/all_to_all | solution.py:20
  212.8 5.2 %all-to-all-done.5 = f32[8,1,4096]{2,1,0:T(1,128)S(1)} async-done(((f32[8,1,4096]{2,1,0:T(1,128)}), f32[8,1,4096]{2,1,0:T(1,128)S(1)}, u32[]{:S(2)}, u32[]{:S(2)}) %all-to-all-start.5) | async-done | bytes 131104 | tf_op jit(solution)/shard_map/all_to_all | solution.py:20
  219.2 5.8 %cholesky.55 = f32[64,64]{1,0:T(8,128)S(1)} custom-call(f32[64,64]{1,0:T(8,128)S(1)} %fusion.23), custom_call_target="Cholesky" | custom-call | tf_op jit(solution)/shard_map/jit(cholesky)/cholesky | solution.py:101
  226.4 4.9 %custom-call.8 = f32[1,64,64]{1,2,0:T(8,128)S(1)} custom-call(f32[1,64,64]{2,1,0:T(8,128)S(1)} %fusion.21), custom_call_target="InvertDiagBlocksLowerTriangular" | custom-call | tf_op jit(solution)/shard_map/jit(_solve_triangular)/triangular_solve | solution.py:102
  (54 shorter events, 24.4 us)
Async XLA Ops:
  7.2 7.0 %copy-start = (bf16[128,64]{0,1:T(8,128)(2,1)S(1)}, bf16[128,64]{0,1:T(8,128)(2,1)}, u32[]{:S(2)}) copy-start(bf16[128,64]{0,1:T(8,128)(2,1)} %param.8) | copy-start | bytes 49156
  7.2 87.7 %all-gather.2.cloned.1.call-start = ((), (), s32[]{:S(2)}) async-start(), calls=%async_computation.6 | async-start | bytes 4325376 | tf_op jit(solution)/shard_map/all_gather | solution.py:77
  9.9 57.6 %all-to-all-start = ((bf16[8,128,512]{2,1,0:T(8,128)(2,1)}), bf16[8,128,512]{2,1,0:T(8,128)(2,1)S(1)}, u32[]{:S(2)}, u32[]{:S(2)}) async-start(bf16[8,128,512]{2,1,0:T(8,128)(2,1)} %broadcast_in_dim.22), calls=%async_computation | async-start | bytes 2097152 | tf_op jit(solution)/shard_map/all_to_all | solution.py:20
  208.6 9.4 %all-to-all-start.5 = ((f32[8,1,4096]{2,1,0:T(1,128)}), f32[8,1,4096]{2,1,0:T(1,128)S(1)}, u32[]{:S(2)}, u32[]{:S(2)}) async-start(f32[8,1,4096]{2,1,0:T(1,128)} %reshape.37), calls=%async_computation.5 | async-start | bytes 262144 | tf_op jit(solution)/shard_map/all_to_all | solution.py:20
Sparse Core Ops, SparseCore 0:
  10.6 84.2 all-gather.1
where the time goes:
time: 240 us; the launch traced here: 239 us
  blocking collectives  118 us (49%)
  other arithmetic  40.8 us (17%)
  waiting for transfers between devices  33 us (14%)
  matrix products  18.2 us (8%)
  between operations  14.3 us (6%)
  starting transfers between devices  7.89 us (3%)
  local copies, waits for them, and re-layouts  6.8 us (3%)
    all_to_all x3, blocking collectives, from_everyone(): return lax.all_to_all(copies, axis, split_axis=0, concat_axis=0, tiled=True)  53.5 us
    all_gather x1, blocking collectives, per_device(): tests = lax.all_gather(sketch, COL, axis=0, tiled=True)  52.8 us
    all_gather x1, waiting for transfers between devices, per_device(): points = lax.all_gather(embeddings, COL, axis=0, tiled=True)  27.1 us
    dot_general x8, matrix products, step(): jnp.dot(tile, block_tests, preferred_element_type=jnp.float32)  16.7 us
    all_to_all x1, blocking collectives, sent_and_summed(): lax.all_to_all(in_blocks(shard, dim, length), axis, 0, 0, tiled=True)  11.6 us
    reduce_sum x9, other arithmetic, squares_of(): return jnp.sum(jnp.square(points.astype(jnp.float32)), axis=1)  10 us
    all_to_all x2, starting transfers between devices, from_everyone(): return lax.all_to_all(copies, axis, split_axis=0, concat_axis=0, tiled=True)  7.85 us
    another operation x3, other arithmetic, per_device(): lower_two = jnp.linalg.cholesky(gram_two)  6.52 us
  transfers between devices with their start and end apart: 3, of which 2 were waited for; matrix products, arithmetic and copies ran while one was open for 1% of the time, Pallas kernels for 0%

commit v1 on v0

--- a/solution.py
+++ b/solution.py
@@ -3,10 +3,16 @@
 from jax import lax
 from jax.sharding import Mesh
 from jax.sharding import PartitionSpec as P
+from jax.lax import all_gather
 
 ROW = ("row_0", "row_1")
 COL = ("col_0", "col_1")
 ROW_COL = ("row_0", "row_1", "col_0", "col_1")
+obtain_row = lambda q_in, m: jnp.split(
+    all_gather(jnp.concatenate([m, q_in], axis=1), axis_name=COL, axis=0, tiled=True),
+    [m.shape[1]],
+    axis=1,
+)
 
 
 def in_order(blocks, dim):
@@ -74,8 +80,7 @@
     own_sq = squares_of(own_points)
     empty = jnp.zeros((own_points.shape[0], sketch.shape[1]), jnp.float32)
     total = empty
-    points = lax.all_gather(embeddings, COL, axis=0, tiled=True)
-    tests = lax.all_gather(sketch, COL, axis=0, tiled=True)
+    points, tests = obtain_row(sketch, embeddings)
     count = points.shape[0]
     size = 512
 

time: 240 us -> 249 us (1.038)
  waiting for transfers between devices: 33 us -> 86.8 us
  blocking collectives: 118 us -> 65.2 us
  local copies, waits for them, and re-layouts: 6.8 us -> 12.9 us
    all_gather x1 -> x0, blocking collectives: 52.8 us -> none  [per_device(): tests = lax.all_gather(sketch, COL, axis=0, tiled=True)]
    all_gather x1, waiting for transfers between devices: 27.1 us -> 65.7 us  [all_gather(jnp.concatenate([m, q_in], axis=1), axis_name=COL, axis=0, til...]
    all_to_all x2, waiting for transfers between devices: 5.23 us -> 21.2 us  [from_everyone(): return lax.all_to_all(copies, axis, split_axis=0, concat_axis=0, tiled=True)]
    split x0 -> x3, local copies, waits for them, and re-layouts: none -> 5.69 us  [jnp.split(all_gather(jnp.concatenate([m, q_in], axis=1), axis_name=COL, a...]
  transfers between devices with their start and end apart: 3 -> 3, of which waited for: 2 -> 3; matrix products, arithmetic and copies ran while one was open for 1% -> 1% of each run, Pallas kernels for 0% -> 0%
where the time goes in v1:
time: 249 us; the launch traced here: 248 us
  waiting for transfers between devices  86.8 us (35%)
  blocking collectives  65.2 us (26%)
  other arithmetic  42.4 us (17%)
  matrix products  18.2 us (7%)
  between operations  14.3 us (6%)
  local copies, waits for them, and re-layouts  12.9 us (5%)
  starting transfers between devices  7.89 us (3%)
    all_gather x1, waiting for transfers between devices, all_gather(jnp.concatenate([m, q_in], axis=1), axis_name=COL, axis=0, til...  65.7 us
    all_to_all x3, blocking collectives, from_everyone(): return lax.all_to_all(copies, axis, split_axis=0, concat_axis=0, tiled=True)  53.6 us
    all_to_all x2, waiting for transfers between devices, from_everyone(): return lax.all_to_all(copies, axis, split_axis=0, concat_axis=0, tiled=True)  21.2 us
    dot_general x8, matrix products, step(): jnp.dot(tile, block_tests, preferred_element_type=jnp.float32)  16.7 us
    all_to_all x1, blocking collectives, sent_and_summed(): lax.all_to_all(in_blocks(shard, dim, length), axis, 0, 0, tiled=True)  11.6 us
    reduce_sum x9, other arithmetic, squares_of(): return jnp.sum(jnp.square(points.astype(jnp.float32)), axis=1)  10 us
    all_to_all x2, starting transfers between devices, from_everyone(): return lax.all_to_all(copies, axis, split_axis=0, concat_axis=0, tiled=True)  7.85 us
    another operation x3, other arithmetic, per_device(): lower = jnp.linalg.cholesky(core)  6.52 us
  transfers between devices with their start and end apart: 3, of which 3 were waited for; matrix products, arithmetic and copies ran while one was open for 1% of the time, Pallas kernels for 0%

profile of v1, /device:TPU:32, one launch (start us, length us, event | category | flops | bytes accessed | tf_op | source)
XLA Modules:
  0.0 247.8 jit_solution(10696623701706578515)
XLA Ops:
  9.7 2.0 broadcast_in_dim.22
  11.7 4.3 %all-to-all-start = ((bf16[8,128,512]{2,1,0:T(8,128)(2,1)}), bf16[8,128,512]{2,1,0:T(8,128)(2,1)S(1)}, u32[]{:S(2)}, u32[]{:S(2)}) async-start(bf16[8,128,512]{2,1,0:T(8,128)(2,1)} %broadcast_in_dim.22), calls=%async_computation | async-start | bytes 2097152 | tf_op jit(solution)/shard_map/all_to_all | solution.py:26
  16.0 15.9 %all-to-all-done = bf16[8,128,512]{2,1,0:T(8,128)(2,1)S(1)} async-done(((bf16[8,128,512]{2,1,0:T(8,128)(2,1)}), bf16[8,128,512]{2,1,0:T(8,128)(2,1)S(1)}, u32[]{:S(2)}, u32[]{:S(2)}) %all-to-all-start) | async-done | bytes 1048608 | tf_op jit(solution)/shard_map/all_to_all | solution.py:26
  32.2 65.7 %all-gather.2.cloned.1.call-done = bf16[4096,576]{1,0:T(8,128)(2,1)} async-done(((bf16[128,576]{1,0:T(8,128)(2,1)}), bf16[4096,576]{1,0:T(8,128)(2,1)}) %all-gather.2.cloned.1.call-update) | async-done | bytes 4718608 | tf_op jit(solution)/shard_map/all_gather | solution.py:12
  97.8 4.5 %split.8 = bf16[4096,512]{1,0:T(8,128)(2,1)} slice(bf16[4096,576]{1,0:T(8,128)(2,1)} %all-gather.2.cloned.1.call-done), slice={[0:4096], [0:512]} | slice | bytes 8388608 | tf_op jit(solution)/shard_map/split | solution.py:11
  103.5 26.7 %while.11 = (s32[]{:T(128)}, f32[1024,64]{0,1:T(8,128)S(1)}, f32[1024]{0:T(1024)S(1)}, bf16[8,512,512]{2,1,0:T(8,128)(2,1)}, bf16[1024,512]{1,0:T(8,128)(2,1)S(1...) while((s32[]{:T(128)}, f32[1024,64]{0,1:T(8,128)S(1)}, f32[1024]{0:T(1024)S(1)}, ...), condition=%wide.region_3.4_spmd.clone, body=%wide.region_1.3_spmd.clone.sunk | while | flops 607518208 | bytes 2761827 | solution.py:96
  104.8 2.1 fusion.45
  108.1 2.1 fusion.45
  111.4 2.1 fusion.45
  114.8 2.1 fusion.45
  118.1 2.1 fusion.45
  121.4 2.1 fusion.45
  124.8 2.1 fusion.45
  128.1 2.1 fusion.45
  130.2 11.6 %all_to_all.30 = f32[8,128,64]{1,2,0:T(8,128)S(1)} all-to-all(f32[8,128,64]{1,2,0:T(8,128)S(1)} %copy_bitcast_fusion), channel_id=1, replica_groups=mesh['row_0'=4,'row_1'=2,'col_0'=4,'col_1'=8] {'row_0','row_1'}, dimensions={0} | all-to-all | bytes 524288 | tf_op jit(solution)/shard_map/all_to_all | solution.py:41
  142.9 23.0 %all_to_all.31 = f32[32,1,4096]{2,1,0:T(1,128)S(1)} all-to-all(f32[32,1,4096]{2,1,0:T(1,128)S(1)} %reshape.31), channel_id=1, replica_groups=mesh['row_0'=4,'row_1'=2,'col_0'=4,'col_1'=8] {'col_0','col_1'}, dimensions={0} | all-to-all | bytes 1048576 | tf_op jit(solution)/shard_map/all_to_all | solution.py:26
  169.0 8.5 %all_to_all.32 = f32[8,1,4096]{2,1,0:T(1,128)S(1)} all-to-all(f32[8,1,4096]{2,1,0:T(1,128)S(1)} %reshape.33), channel_id=1, replica_groups=mesh['row_0'=4,'row_1'=2,'col_0'=4,'col_1'=8] {'row_0','row_1'}, dimensions={0} | all-to-all | bytes 262144 | tf_op jit(solution)/shard_map/all_to_all | solution.py:26
  178.7 5.8 %cholesky.44 = f32[64,64]{1,0:T(8,128)S(1)} custom-call(f32[64,64]{1,0:T(8,128)S(1)} %fusion.27), custom_call_target="Cholesky" | custom-call | tf_op jit(solution)/shard_map/jit(cholesky)/cholesky | solution.py:101
  185.9 4.9 %custom-call.7 = f32[1,64,64]{1,2,0:T(8,128)S(1)} custom-call(f32[1,64,64]{2,1,0:T(8,128)S(1)} %fusion.20), custom_call_target="InvertDiagBlocksLowerTriangular" | custom-call | tf_op jit(solution)/shard_map/jit(_solve_triangular)/triangular_solve | solution.py:102
  192.0 22.1 %all_to_all.33 = f32[32,1,4096]{2,1,0:T(1,128)S(1)} all-to-all(f32[32,1,4096]{2,1,0:T(1,128)S(1)} %reshape.35), channel_id=1, replica_groups=mesh['row_0'=4,'row_1'=2,'col_0'=4,'col_1'=8] {'col_0','col_1'}, dimensions={0} | all-to-all | bytes 1048576 | tf_op jit(solution)/shard_map/all_to_all | solution.py:26
  217.4 3.5 %all-to-all-start.5 = ((f32[8,1,4096]{2,1,0:T(1,128)}), f32[8,1,4096]{2,1,0:T(1,128)S(1)}, u32[]{:S(2)}, u32[]{:S(2)}) async-start(f32[8,1,4096]{2,1,0:T(1,128)} %reshape.37), calls=%async_computation.5 | async-start | bytes 262144 | tf_op jit(solution)/shard_map/all_to_all | solution.py:26
  221.6 5.2 %all-to-all-done.5 = f32[8,1,4096]{2,1,0:T(1,128)S(1)} async-done(((f32[8,1,4096]{2,1,0:T(1,128)}), f32[8,1,4096]{2,1,0:T(1,128)S(1)}, u32[]{:S(2)}, u32[]{:S(2)}) %all-to-all-start.5) | async-done | bytes 131104 | tf_op jit(solution)/shard_map/all_to_all | solution.py:26
  228.0 5.8 %cholesky.55 = f32[64,64]{1,0:T(8,128)S(1)} custom-call(f32[64,64]{1,0:T(8,128)S(1)} %fusion.23), custom_call_target="Cholesky" | custom-call | tf_op jit(solution)/shard_map/jit(cholesky)/cholesky | solution.py:106
  235.2 4.9 %custom-call.8 = f32[1,64,64]{1,2,0:T(8,128)S(1)} custom-call(f32[1,64,64]{2,1,0:T(8,128)S(1)} %fusion.21), custom_call_target="InvertDiagBlocksLowerTriangular" | custom-call | tf_op jit(solution)/shard_map/jit(_solve_triangular)/triangular_solve | solution.py:107
  (57 shorter events, 28.8 us)
Async XLA Ops:
  7.2 90.7 %all-gather.2.cloned.1.call-start = ((), (), s32[]{:S(2)}) async-start(), calls=%async_computation.6 | async-start | bytes 5406720 | tf_op jit(solution)/shard_map/all_gather | solution.py:12
  11.7 20.2 %all-to-all-start = ((bf16[8,128,512]{2,1,0:T(8,128)(2,1)}), bf16[8,128,512]{2,1,0:T(8,128)(2,1)S(1)}, u32[]{:S(2)}, u32[]{:S(2)}) async-start(bf16[8,128,512]{2,1,0:T(8,128)(2,1)} %broadcast_in_dim.22), calls=%async_computation | async-start | bytes 2097152 | tf_op jit(solution)/shard_map/all_to_all | solution.py:26
  102.3 1.2 slice-start
  103.5 38.3 %copy-start = (bf16[128,64]{0,1:T(8,128)(2,1)S(1)}, bf16[128,64]{0,1:T(8,128)(2,1)}, u32[]{:S(2)}) copy-start(bf16[128,64]{0,1:T(8,128)(2,1)} %param.8) | copy-start | bytes 49156
  217.4 9.4 %all-to-all-start.5 = ((f32[8,1,4096]{2,1,0:T(1,128)}), f32[8,1,4096]{2,1,0:T(1,128)S(1)}, u32[]{:S(2)}, u32[]{:S(2)}) async-start(f32[8,1,4096]{2,1,0:T(1,128)} %reshape.37), calls=%async_computation.5 | async-start | bytes 262144 | tf_op jit(solution)/shard_map/all_to_all | solution.py:26
Sparse Core Ops, SparseCore 0:
  10.5 87.2 all-gather.1
